TPU v7x, 256 devices: a whole 4x4x8 slice. The times are simulated.
256 devices in a mesh: src: 16 (over x_hi, z), tgt: 16 (over x_lo, y, core).
Axes of the slice: x: 4 (x_hi: 2, x_lo: 2; x = x_hi * 2 + x_lo), y: 4, z: 8, core: 2. Of those that a mesh axis runs over, the one named last changes fastest.
Arguments:
- source_words: bfloat16 [32768, 300], P(('src', 'tgt')), may hold values from -3 to 3
- target_words: bfloat16 [30720, 300], P(('tgt', 'src')), may hold values from -24 to 24
Outputs:
- rotated: bfloat16 [32768, 300], P(('src', 'tgt'))
- matched: float32 [32768, 300], P(('src', 'tgt'))
- ortho: float32 [300, 300], replicated
- row_pot: float32 [32768], P(('src', 'tgt'))
- col_pot: float32 [30720], P(('tgt', 'src'))
All inputs are finite; a program needn't handle non-finite values.
Results may differ from a plain program's by a relative error of at most 0.0034.
Values may be sent and summed in bfloat16 or wider, within the bound.
A program may use at most 64 MiB of HBM per device.

v0:
```python
import math
import jax
import jax.numpy as jnp
from jax import lax
from jax.sharding import PartitionSpec as P

ITERS = 2
NEWTON = 12


def sent_to_all(array, axis):
    copies = jnp.broadcast_to(array, (lax.axis_size(axis), *array.shape))
    return lax.all_to_all(copies, axis, split_axis=0, concat_axis=0, tiled=True)


def collected_together(array, axis):
    leaves = jax.tree.leaves(array)
    sequence = sorted(range(len(leaves)), key=lambda k: -leaves[k].size)
    width = (1, *leaves[sequence[0]].shape)[-1]
    lines = [
        jnp.pad(leaves[k].reshape(-1), (0, -leaves[k].size % width)).reshape(-1, width)
        for k in sequence
    ]
    both, at, found = (sent_to_all(jnp.concatenate(lines), axis), 0, {})
    for k, line in zip(sequence, lines):
        share = both[:, at : at + len(line)].reshape(len(both), -1)
        found[k] = share[:, : leaves[k].size].reshape(-1, *leaves[k].shape)
        at += len(line)
    numbers = iter(range(len(leaves)))
    return jax.tree.map(lambda _: found[next(numbers)], array)


def folded_in_pairs(pieces, combine):
    while len(jax.tree.leaves(pieces)[0]) > 1:
        pieces = jax.vmap(combine)(
            *(jax.tree.map(lambda part: part[side::2], pieces) for side in (0, 1))
        )
    return jax.tree.map(lambda part: part[0], pieces)


def combined_all(array, axis, combine):
    pieces = collected_together(array, axis)
    return folded_in_pairs(pieces, combine)


def gathered_by_type(array, axis):
    leaves, found = (jax.tree.leaves(array), {})
    for first, a in enumerate(leaves):
        if first not in found:
            alike = [k for k, b in enumerate(leaves) if b.dtype == a.dtype]
            got = (
                collected_together([leaves[k] for k in alike], axis)
                if len(alike) > 1
                else [sent_to_all(a, axis)]
            )
            for k, b in zip(alike, got):
                found[k] = b
    numbers = iter(range(len(leaves)))
    return jax.tree.map(lambda _: found[next(numbers)], array)


def combined_all_2(array, axis, combine):
    pieces = gathered_by_type(array, axis)
    return folded_in_pairs(pieces, combine)


def joined_along(blocks, dim):
    lengths = list(blocks.shape[1:])
    lengths[dim] *= blocks.shape[0]
    return jnp.moveaxis(blocks, 0, dim).reshape(lengths)


def collect(array, axis, dim):
    return joined_along(sent_to_all(array, axis), dim)


def split_up(array, dim, size):
    lengths = array.shape
    blocks = array.reshape(*lengths[:dim], size, lengths[dim] // size, *lengths[dim + 1 :])
    return jnp.moveaxis(blocks, dim, 0)


def summed_on_arrival(array, axis, dim):
    blocks = split_up(array, dim, lax.axis_size(axis))
    arrived = lax.all_to_all(blocks, axis, split_axis=0, concat_axis=0, tiled=True)
    return arrived.sum(axis=0)


def combine(first, second):
    higher = jnp.maximum(first[0], second[0])
    return (higher, first[1] * jnp.exp(first[0] - higher) + second[1] * jnp.exp(second[0] - higher))


def reduce_rows(top, total):
    higher, whole = combined_all((top, total), "tgt", combine)
    return -(higher + jnp.log(whole))


def reduce_cols(top, total):
    higher, whole = combined_all_2((top, total), "src", combine)
    return -(higher + jnp.log(whole))


def body(source_words, target_words):
    width = source_words.shape[1]
    scale = 4.0 / math.sqrt(width)
    highest = lax.Precision.HIGHEST
    src_block = collect(source_words, "tgt", 0)
    rows = src_block.shape[0]
    cols = target_words.shape[0] * lax.axis_size("src")
    inner = (((1,), (1,)), ((), ()))
    leading = (((0,), (0,)), ((), ()))

    def scores(piece):
        return lax.dot_general(src_block, piece, inner, preferred_element_type=jnp.float32) * scale

    col_pot = jnp.zeros((cols,), jnp.float32)
    row_pot = jnp.zeros((rows,), jnp.float32)
    for sweep_index in range(ITERS):
        row_top = jnp.full((rows,), -jnp.inf, jnp.float32)
        total = jnp.zeros((rows,), jnp.float32)
        row_shift = col_pot
        row_logits = scores(collect(target_words, "src", 0)) + row_shift[None, :]
        higher = jnp.maximum(row_top, jnp.max(row_logits, axis=1))
        total = total * jnp.exp(row_top - higher) + jnp.sum(
            jnp.exp(row_logits - higher[:, None]), axis=1
        )
        top, total = (higher, total)
        row_pot = reduce_rows(top, total)
        logits = scores(collect(target_words, "src", 0)) + row_pot[:, None]
        col_top = jnp.max(logits, axis=0)
        parts = jnp.stack([col_top, jnp.sum(jnp.exp(logits - col_top[None, :]), axis=0)])
        col_pot = reduce_cols(parts[0], parts[1])
    piece = collect(target_words, "src", 0)
    plan = jnp.exp(scores(piece) + row_pot[:, None] + col_pot[None, :]).astype(jnp.bfloat16)
    summed = jnp.dot(plan, piece, preferred_element_type=jnp.float32)
    matched = summed_on_arrival(summed, "tgt", 0)
    term = lax.dot_general(src_block.astype(jnp.float32), summed, leading, precision=highest)
    cov = lax.psum(term, ("src", "tgt"))
    ortho = cov / jnp.sqrt(jnp.sum(cov * cov) + 1e-06)
    for step_index in range(NEWTON):
        ortho = 1.5 * ortho - 0.5 * jnp.dot(
            ortho, jnp.dot(ortho.T, ortho, precision=highest), precision=highest
        )
    rotated = jnp.dot(source_words.astype(jnp.float32), ortho, precision=highest).astype(
        jnp.bfloat16
    )
    own_rows = rows // lax.axis_size("tgt")
    own_cols = cols // lax.axis_size("src")
    row_part = lax.dynamic_slice_in_dim(row_pot, lax.axis_index("tgt") * own_rows, own_rows)
    col_part = lax.dynamic_slice_in_dim(col_pot, lax.axis_index("src") * own_cols, own_cols)
    return (rotated, matched, ortho, row_part, col_part)


def solution(mesh):
    in_specs = (P(("src", "tgt"), None), P(("tgt", "src"), None))
    out_specs = (
        P(("src", "tgt"), None),
        P(("src", "tgt"), None),
        P(),
        P(("src", "tgt")),
        P(("tgt", "src")),
    )
    return jax.shard_map(body, mesh=mesh, in_specs=in_specs, out_specs=out_specs, check_vma=False)
```

profile of v0, /device:TPU:2, one launch (start us, length us, event | category | flops | bytes accessed | tf_op | source)
XLA Modules:
  0.0 516.1 jit_solution(17925122348003594462)
XLA Ops:
  8.2 23.0 %all_to_all.39 = bf16[16,128,300]{1,2,0:T(8,128)(2,1)S(1)} all-to-all(bf16[16,128,300]{1,2,0:T(8,128)(2,1)S(1)} %broadcast_in_dim.12), channel_id=1, replica_groups=mesh['src'=16,'tgt'=16] {'tgt'}, dimensions={0} | all-to-all | bytes 2457600 | tf_op jit(solution)/shard_map/all_to_all | solution.py:13
  33.3 10.1 %all-to-all-start.1 = ((bf16[16,120,300]{1,2,0:T(8,128)(2,1)}), bf16[16,120,300]{1,2,0:T(8,128)(2,1)S(1)}, u32[]{:S(2)}, u32[]{:S(2)}) async-start(bf16[16,120,300]{1,2,0:T(8,128)(2,1)} %broadcast_in_dim.13), calls=%async_computation.1 | async-start | bytes 2490368 | tf_op jit(solution)/shard_map/all_to_all | solution.py:13
  44.3 32.0 %all-to-all-done.1 = bf16[16,120,300]{1,2,0:T(8,128)(2,1)S(1)} async-done(((bf16[16,120,300]{1,2,0:T(8,128)(2,1)}), bf16[16,120,300]{1,2,0:T(8,128)(2,1)S(1)}, u32[]{:S(2)}, u32[]{:S(2)}) %all-to-all-start.1) | async-done | bytes 1152032 | tf_op jit(solution)/shard_map/all_to_all | solution.py:13
  77.7 2.7 reshape.145
  80.5 8.0 %fusion.30 = (f32[2048]{0:T(1024)S(1)}, f32[2048,1920]{1,0:T(8,128)}) fusion(bf16[2048,300]{0,1:T(8,128)(2,1)S(1)} %bitcast.103, bf16[1920,300]{0,1:T(8,128)(2,1)S(1)} %reshape.145), kind=kOutput, calls=%fused_computation.101 | convolution fusion | flops 2367158272 | bytes 18117632 | tf_op jit(solution)/shard_map/dot_general | solution.py:115
  88.4 7.7 %exponential_reduce_fusion.3 = f32[2048]{0:T(1024)S(1)} fusion(f32[2048,1920]{1,0:T(8,128)} %get-tuple-element.55, f32[2048]{0:T(1024)S(1)} %get-tuple-element.54), kind=kLoop, calls=%fused_computation.4 | loop fusion | flops 7862272 | bytes 15745024 | tf_op jit(solution)/shard_map/reduce_sum | solution.py:125
  96.2 11.4 %all_to_all.40 = f32[16,2,2048]{2,1,0:T(2,128)S(1)} all-to-all(f32[16,2,2048]{2,1,0:T(2,128)S(1)} %broadcast_in_dim.14), channel_id=1, replica_groups=mesh['src'=16,'tgt'=16] {'tgt'}, dimensions={0} | all-to-all | bytes 524288 | tf_op jit(solution)/shard_map/all_to_all | solution.py:13
  108.5 6.6 %add_reduce_fusion.1 = f32[1920]{0:T(1024)S(1)} fusion(f32[2048,1920]{1,0:T(8,128)} %get-tuple-element.55, f32[2048]{0:T(1024)S(1)} %bitcast.127), kind=kLoop, calls=%fused_computation.6 | loop fusion | flops 7862400 | bytes 15744512 | tf_op jit(solution)/shard_map/reduce_max | solution.py:131
  115.0 8.1 %exponential_reduce_fusion.2 = f32[1920]{0:T(1024)S(1)} fusion(f32[2048,1920]{1,0:T(8,128)} %get-tuple-element.55, f32[1920]{0:T(1024)S(1)} %add_reduce_fusion.1, f32[2048]{0:T(1024)S(1)} %bitcast.128), kind=kLoop, calls=%fused_computation.3 | loop fusion | flops 11794560 | bytes 15752192 | tf_op jit(solution)/shard_map/reduce_sum | solution.py:132
  123.3 15.1 %all_to_all.41 = f32[16,2,1920]{2,1,0:T(2,128)S(1)} all-to-all(f32[16,2,1920]{2,1,0:T(2,128)S(1)} %broadcast_in_dim.15), channel_id=1, replica_groups=mesh['src'=16,'tgt'=16] {'src'}, dimensions={0} | all-to-all | bytes 491520 | tf_op jit(solution)/shard_map/all_to_all | solution.py:13
  139.2 6.6 %add_reduce_fusion = f32[2048]{0:T(1024)S(1)} fusion(f32[2048,1920]{1,0:T(8,128)} %get-tuple-element.55, f32[1920]{0:T(1024)S(1)} %negate_reduce_fusion), kind=kLoop, calls=%fused_computation.5 | loop fusion | flops 7862272 | bytes 15744512 | tf_op jit(solution)/shard_map/reduce_max | solution.py:124
  145.7 8.2 %exponential_reduce_fusion.1 = f32[2048]{0:T(1024)S(1)} fusion(f32[2048,1920]{1,0:T(8,128)} %get-tuple-element.55, f32[2048]{0:T(1024)S(1)} %add_reduce_fusion, f32[1920]{0:T(1024)S(1)} %negate_reduce_fusion), kind=kLoop, calls=%fused_computation.2 | loop fusion | flops 11794432 | bytes 15752704 | tf_op jit(solution)/shard_map/reduce_sum | solution.py:125
  154.1 11.6 %all_to_all.42 = f32[16,2,2048]{2,1,0:T(2,128)S(1)} all-to-all(f32[16,2,2048]{2,1,0:T(2,128)S(1)} %broadcast_in_dim.16), channel_id=1, replica_groups=mesh['src'=16,'tgt'=16] {'tgt'}, dimensions={0} | all-to-all | bytes 524288 | tf_op jit(solution)/shard_map/all_to_all | solution.py:13
  166.5 6.6 %add_reduce_fusion.2 = f32[1920]{0:T(1024)S(1)} fusion(f32[2048,1920]{1,0:T(8,128)} %get-tuple-element.55, f32[2048]{0:T(1024)S(1)} %bitcast.124), kind=kLoop, calls=%fused_computation.7 | loop fusion | flops 7862400 | bytes 15744512 | tf_op jit(solution)/shard_map/reduce_max | solution.py:131
  173.1 8.1 %exponential_reduce_fusion = f32[1920]{0:T(1024)S(1)} fusion(f32[2048,1920]{1,0:T(8,128)} %get-tuple-element.55, f32[1920]{0:T(1024)S(1)} %add_reduce_fusion.2, f32[2048]{0:T(1024)S(1)} %bitcast.125), kind=kLoop, calls=%fused_computation.1 | loop fusion | flops 11794560 | bytes 15752192 | tf_op jit(solution)/shard_map/reduce_sum | solution.py:132
  182.1 4.3 all-to-all-start.5
  186.9 10.8 %all-to-all-done.5 = f32[16,2,1920]{2,1,0:T(2,128)S(1)} async-done(((f32[16,2,1920]{2,1,0:T(2,128)}), f32[16,2,1920]{2,1,0:T(2,128)S(1)}, u32[]{:S(2)}, u32[]{:S(2)}) %all-to-all-start.5) | async-done | bytes 245792 | tf_op jit(solution)/shard_map/all_to_all | solution.py:13
  198.5 9.8 %fusion = f32[2048,300]{0,1:T(8,128)} fusion(bf16[1920,300]{0,1:T(8,128)(2,1)S(1)} %reshape.145, f32[2048,1920]{1,0:T(8,128)} %get-tuple-element.55, f32[1920]{0:T(1024)S(1)} %get-tuple-element.20, f32[2048]{0:T(1024)S(1)} %bitcast.126), kind=kOutput, calls=%fused_computation.9 | convolution fusion | flops 2371092480 | bytes 19354112 | tf_op jit(solution)/shard_map/dot_general | solution.py:136
  208.3 4.6 convolution_bitcast_fusion
  215.2 2.2 copy.60
  217.4 4.9 all-to-all-start.6
  222.9 250.2 %all-reduce.2.cloned.1.call-done = f32[300,300]{0,1:T(8,128)} async-done(((f32[300,300]{0,1:T(8,128)}), f32[300,300]{0,1:T(8,128)}) %all-reduce.2.cloned.1.call-update) | async-done | bytes 360016 | tf_op jit(solution)/shard_map/psum | solution.py:139
  475.6 2.2 fusion.16
  477.8 2.4 fusion.14
  (130 shorter events, 43.1 us)
Async XLA Ops:
  33.3 43.0 %all-to-all-start.1 = ((bf16[16,120,300]{1,2,0:T(8,128)(2,1)}), bf16[16,120,300]{1,2,0:T(8,128)(2,1)S(1)}, u32[]{:S(2)}, u32[]{:S(2)}) async-start(bf16[16,120,300]{1,2,0:T(8,128)(2,1)} %broadcast_in_dim.13), calls=%async_computation.1 | async-start | bytes 2490368 | tf_op jit(solution)/shard_map/all_to_all | solution.py:13
  182.1 15.6 %all-to-all-start.5 = ((f32[16,2,1920]{2,1,0:T(2,128)}), f32[16,2,1920]{2,1,0:T(2,128)S(1)}, u32[]{:S(2)}, u32[]{:S(2)}) async-start(f32[16,2,1920]{2,1,0:T(2,128)} %broadcast_in_dim.17), calls=%async_computation.5 | async-start | bytes 491520 | tf_op jit(solution)/shard_map/all_to_all | solution.py:13
  186.4 286.8 %all-reduce.2.cloned.1.call-start = ((), (), s32[]{:S(2)}) async-start(), calls=%async_computation.7 | async-start | bytes 933888 | tf_op jit(solution)/shard_map/psum | solution.py:139
  217.4 290.6 %all-to-all-start.6 = ((f32[16,128,300]{1,2,0:T(8,128)}), f32[16,128,300]{1,2,0:T(8,128)S(1)}, u32[]{:S(2)}, u32[]{:S(2)}) async-start(f32[16,128,300]{1,2,0:T(8,128)} %copy.60), calls=%async_computation.6 | async-start | bytes 4980736 | tf_op jit(solution)/shard_map/all_to_all | solution.py:85
  480.2 26.8 %copy-start = (bf16[128,300]{0,1:T(8,128)(2,1)S(1)}, bf16[128,300]{0,1:T(8,128)(2,1)}, u32[]{:S(2)}) copy-start(bf16[128,300]{0,1:T(8,128)(2,1)} %param.2) | copy-start | bytes 230404
Sparse Core Ops, SparseCore 0:
  213.0 260.1 all-reduce.1
where the time goes:
time: 523 us; the launch traced here: 516 us
  waiting for transfers between devices  293 us (56%)
  blocking collectives  61.2 us (12%)
  other arithmetic  55 us (11%)
  matrix products  53.5 us (10%)
  starting transfers between devices  19.4 us (4%)
  local copies, waits for them, and re-layouts  18.1 us (3%)
  between operations  15.8 us (3%)
    psum x1, waiting for transfers between devices, body(): cov = lax.psum(term, ('src', 'tgt'))  250 us
    all_to_all x4, blocking collectives, sent_to_all(): return lax.all_to_all(copies, axis, split_axis=0, concat_axis=0, tiled=True)  61.2 us
    all_to_all x2, waiting for transfers between devices, sent_to_all(): return lax.all_to_all(copies, axis, split_axis=0, concat_axis=0, tiled=True)  42.8 us
    dot_general x12, matrix products, body(): jnp.dot(ortho, jnp.dot(ortho.T, ortho, precision=highest), precision=high...  16.4 us
    reduce_sum x2, other arithmetic, body(): jnp.sum(jnp.exp(logits - col_top[None, :]), axis=0)  16.2 us
    reduce_sum x2, other arithmetic, body(): jnp.sum(jnp.exp(row_logits - higher[:, None]), axis=1)  15.8 us
    all_to_all x2, starting transfers between devices, sent_to_all(): return lax.all_to_all(copies, axis, split_axis=0, concat_axis=0, tiled=True)  14.4 us
    dot_general x12, matrix products, body(): jnp.dot(ortho.T, ortho, precision=highest)  13.8 us
  transfers between devices with their start and end apart: 4, of which 3 were waited for; matrix products, arithmetic and copies ran while one was open for 8% of the time, Pallas kernels for 0%

commit v1 on v0

--- a/solution.py
+++ b/solution.py
@@ -136,7 +136,9 @@
     summed = jnp.dot(plan, piece, preferred_element_type=jnp.float32)
     matched = summed_on_arrival(summed, "tgt", 0)
     term = lax.dot_general(src_block.astype(jnp.float32), summed, leading, precision=highest)
-    cov = lax.psum(term, ("src", "tgt"))
+    cov = term
+    for over in ("tgt", "src"):
+        cov = lax.psum(cov, over)
     ortho = cov / jnp.sqrt(jnp.sum(cov * cov) + 1e-06)
     for step_index in range(NEWTON):
         ortho = 1.5 * ortho - 0.5 * jnp.dot(

time: 523 us -> 541 us (1.034)
  blocking collectives: 61.2 us -> 76.6 us
  waiting for transfers between devices: 293 us -> 299 us
    psum x1 -> x2, waiting for transfers between devices: 250 us -> 267 us  [body(): cov = lax.psum(cov, over)]
    all_to_all x4 -> x5, blocking collectives: 61.2 us -> 76.6 us  [sent_to_all(): return lax.all_to_all(copies, axis, split_axis=0, concat_axis=0, tiled=True)]
    all_to_all x2 -> x1, waiting for transfers between devices: 42.8 us -> 32 us  [sent_to_all(): return lax.all_to_all(copies, axis, split_axis=0, concat_axis=0, tiled=True)]
    all_to_all x2 -> x1, starting transfers between devices: 14.4 us -> 10.1 us  [sent_to_all(): return lax.all_to_all(copies, axis, split_axis=0, concat_axis=0, tiled=True)]
where the time goes in v1:
time: 541 us; the launch traced here: 533 us
  waiting for transfers between devices  299 us (55%)
  blocking collectives  76.6 us (14%)
  other arithmetic  55 us (10%)
  matrix products  53.5 us (10%)
  local copies, waits for them, and re-layouts  17.4 us (3%)
  between operations  15.8 us (3%)
  starting transfers between devices  15.2 us (3%)
    psum x2, waiting for transfers between devices, body(): cov = lax.psum(cov, over)  267 us
    all_to_all x5, blocking collectives, sent_to_all(): return lax.all_to_all(copies, axis, split_axis=0, concat_axis=0, tiled=True)  76.6 us
    all_to_all x1, waiting for transfers between devices, sent_to_all(): return lax.all_to_all(copies, axis, split_axis=0, concat_axis=0, tiled=True)  32 us
    dot_general x12, matrix products, body(): jnp.dot(ortho, jnp.dot(ortho.T, ortho, precision=highest), precision=high...  16.4 us
    reduce_sum x2, other arithmetic, body(): jnp.sum(jnp.exp(logits - col_top[None, :]), axis=0)  16.2 us
    reduce_sum x2, other arithmetic, body(): jnp.sum(jnp.exp(row_logits - higher[:, None]), axis=1)  15.8 us
    dot_general x12, matrix products, body(): jnp.dot(ortho.T, ortho, precision=highest)  13.8 us
    reduce_max x2, other arithmetic, body(): col_top = jnp.max(logits, axis=0)  13.1 us
  transfers between devices with their start and end apart: 4, of which 3 were waited for; matrix products, arithmetic and copies ran while one was open for 8% of the time, Pallas kernels for 0%

profile of v1, /device:TPU:2, one launch (start us, length us, event | category | flops | bytes accessed | tf_op | source)
XLA Modules:
  0.0 533.0 jit_solution(13960925923211708584)
XLA Ops:
  8.2 23.0 %all_to_all.39 = bf16[16,128,300]{1,2,0:T(8,128)(2,1)S(1)} all-to-all(bf16[16,128,300]{1,2,0:T(8,128)(2,1)S(1)} %broadcast_in_dim.12), channel_id=1, replica_groups=mesh['src'=16,'tgt'=16] {'tgt'}, dimensions={0} | all-to-all | bytes 2457600 | tf_op jit(solution)/shard_map/all_to_all | solution.py:13
  33.3 10.1 %all-to-all-start.1 = ((bf16[16,120,300]{1,2,0:T(8,128)(2,1)}), bf16[16,120,300]{1,2,0:T(8,128)(2,1)S(1)}, u32[]{:S(2)}, u32[]{:S(2)}) async-start(bf16[16,120,300]{1,2,0:T(8,128)(2,1)} %broadcast_in_dim.13), calls=%async_computation.1 | async-start | bytes 2490368 | tf_op jit(solution)/shard_map/all_to_all | solution.py:13
  44.4 32.0 %all-to-all-done.1 = bf16[16,120,300]{1,2,0:T(8,128)(2,1)S(1)} async-done(((bf16[16,120,300]{1,2,0:T(8,128)(2,1)}), bf16[16,120,300]{1,2,0:T(8,128)(2,1)S(1)}, u32[]{:S(2)}, u32[]{:S(2)}) %all-to-all-start.1) | async-done | bytes 1152032 | tf_op jit(solution)/shard_map/all_to_all | solution.py:13
  77.7 2.7 reshape.145
  80.5 8.0 %fusion.30 = (f32[2048]{0:T(1024)S(1)}, f32[2048,1920]{1,0:T(8,128)}) fusion(bf16[2048,300]{0,1:T(8,128)(2,1)S(1)} %bitcast.103, bf16[1920,300]{0,1:T(8,128)(2,1)S(1)} %reshape.145), kind=kOutput, calls=%fused_computation.101 | convolution fusion | flops 2367158272 | bytes 18117632 | tf_op jit(solution)/shard_map/dot_general | solution.py:115
  88.4 7.7 %exponential_reduce_fusion.3 = f32[2048]{0:T(1024)S(1)} fusion(f32[2048,1920]{1,0:T(8,128)} %get-tuple-element.55, f32[2048]{0:T(1024)S(1)} %get-tuple-element.54), kind=kLoop, calls=%fused_computation.4 | loop fusion | flops 7862272 | bytes 15745024 | tf_op jit(solution)/shard_map/reduce_sum | solution.py:125
  96.2 11.4 %all_to_all.40 = f32[16,2,2048]{2,1,0:T(2,128)S(1)} all-to-all(f32[16,2,2048]{2,1,0:T(2,128)S(1)} %broadcast_in_dim.14), channel_id=1, replica_groups=mesh['src'=16,'tgt'=16] {'tgt'}, dimensions={0} | all-to-all | bytes 524288 | tf_op jit(solution)/shard_map/all_to_all | solution.py:13
  108.5 6.6 %add_reduce_fusion.1 = f32[1920]{0:T(1024)S(1)} fusion(f32[2048,1920]{1,0:T(8,128)} %get-tuple-element.55, f32[2048]{0:T(1024)S(1)} %bitcast.127), kind=kLoop, calls=%fused_computation.6 | loop fusion | flops 7862400 | bytes 15744512 | tf_op jit(solution)/shard_map/reduce_max | solution.py:131
  115.0 8.1 %exponential_reduce_fusion.2 = f32[1920]{0:T(1024)S(1)} fusion(f32[2048,1920]{1,0:T(8,128)} %get-tuple-element.55, f32[1920]{0:T(1024)S(1)} %add_reduce_fusion.1, f32[2048]{0:T(1024)S(1)} %bitcast.128), kind=kLoop, calls=%fused_computation.3 | loop fusion | flops 11794560 | bytes 15752192 | tf_op jit(solution)/shard_map/reduce_sum | solution.py:132
  123.3 15.1 %all_to_all.41 = f32[16,2,1920]{2,1,0:T(2,128)S(1)} all-to-all(f32[16,2,1920]{2,1,0:T(2,128)S(1)} %broadcast_in_dim.15), channel_id=1, replica_groups=mesh['src'=16,'tgt'=16] {'src'}, dimensions={0} | all-to-all | bytes 491520 | tf_op jit(solution)/shard_map/all_to_all | solution.py:13
  139.2 6.6 %add_reduce_fusion = f32[2048]{0:T(1024)S(1)} fusion(f32[2048,1920]{1,0:T(8,128)} %get-tuple-element.55, f32[1920]{0:T(1024)S(1)} %negate_reduce_fusion), kind=kLoop, calls=%fused_computation.5 | loop fusion | flops 7862272 | bytes 15744512 | tf_op jit(solution)/shard_map/reduce_max | solution.py:124
  145.7 8.2 %exponential_reduce_fusion.1 = f32[2048]{0:T(1024)S(1)} fusion(f32[2048,1920]{1,0:T(8,128)} %get-tuple-element.55, f32[2048]{0:T(1024)S(1)} %add_reduce_fusion, f32[1920]{0:T(1024)S(1)} %negate_reduce_fusion), kind=kLoop, calls=%fused_computation.2 | loop fusion | flops 11794432 | bytes 15752704 | tf_op jit(solution)/shard_map/reduce_sum | solution.py:125
  154.1 11.6 %all_to_all.42 = f32[16,2,2048]{2,1,0:T(2,128)S(1)} all-to-all(f32[16,2,2048]{2,1,0:T(2,128)S(1)} %broadcast_in_dim.16), channel_id=1, replica_groups=mesh['src'=16,'tgt'=16] {'tgt'}, dimensions={0} | all-to-all | bytes 524288 | tf_op jit(solution)/shard_map/all_to_all | solution.py:13
  166.5 6.6 %add_reduce_fusion.2 = f32[1920]{0:T(1024)S(1)} fusion(f32[2048,1920]{1,0:T(8,128)} %get-tuple-element.55, f32[2048]{0:T(1024)S(1)} %bitcast.124), kind=kLoop, calls=%fused_computation.7 | loop fusion | flops 7862400 | bytes 15744512 | tf_op jit(solution)/shard_map/reduce_max | solution.py:131
  173.1 8.1 %exponential_reduce_fusion = f32[1920]{0:T(1024)S(1)} fusion(f32[2048,1920]{1,0:T(8,128)} %get-tuple-element.55, f32[1920]{0:T(1024)S(1)} %add_reduce_fusion.2, f32[2048]{0:T(1024)S(1)} %bitcast.125), kind=kLoop, calls=%fused_computation.1 | loop fusion | flops 11794560 | bytes 15752192 | tf_op jit(solution)/shard_map/reduce_sum | solution.py:132
  181.4 15.4 %all_to_all.43 = f32[16,2,1920]{2,1,0:T(2,128)S(1)} all-to-all(f32[16,2,1920]{2,1,0:T(2,128)S(1)} %broadcast_in_dim.17), channel_id=1, replica_groups=mesh['src'=16,'tgt'=16] {'src'}, dimensions={0} | all-to-all | bytes 491520 | tf_op jit(solution)/shard_map/all_to_all | solution.py:13
  197.6 9.8 %fusion = f32[2048,300]{0,1:T(8,128)} fusion(bf16[1920,300]{0,1:T(8,128)(2,1)S(1)} %reshape.145, f32[2048,1920]{1,0:T(8,128)} %get-tuple-element.55, f32[1920]{0:T(1024)S(1)} %get-tuple-element.20, f32[2048]{0:T(1024)S(1)} %bitcast.126), kind=kOutput, calls=%fused_computation.9 | convolution fusion | flops 2371092480 | bytes 19354112 | tf_op jit(solution)/shard_map/dot_general | solution.py:136
  207.4 4.6 convolution_bitcast_fusion
  214.7 115.1 %all-reduce.3.cloned.1.call-done = f32[300,300]{0,1:T(8,128)} async-done(((f32[300,300]{0,1:T(8,128)}), f32[300,300]{0,1:T(8,128)}) %all-reduce.3.cloned.1.call-update) | async-done | bytes 360016 | tf_op jit(solution)/shard_map/psum | solution.py:141
  330.0 2.2 copy.60
  332.2 5.0 all-to-all-start.6
  337.8 152.2 %all-reduce.5.cloned.1.call-done = f32[300,300]{0,1:T(8,128)} async-done(((f32[300,300]{0,1:T(8,128)}), f32[300,300]{0,1:T(8,128)}) %all-reduce.5.cloned.1.call-update) | async-done | bytes 360016 | tf_op jit(solution)/shard_map/psum | solution.py:141
  492.5 2.2 fusion.16
  494.7 2.4 fusion.14
  (132 shorter events, 42.5 us)
Async XLA Ops:
  33.3 43.0 %all-to-all-start.1 = ((bf16[16,120,300]{1,2,0:T(8,128)(2,1)}), bf16[16,120,300]{1,2,0:T(8,128)(2,1)S(1)}, u32[]{:S(2)}, u32[]{:S(2)}) async-start(bf16[16,120,300]{1,2,0:T(8,128)(2,1)} %broadcast_in_dim.13), calls=%async_computation.1 | async-start | bytes 2490368 | tf_op jit(solution)/shard_map/all_to_all | solution.py:13
  43.4 286.3 %all-reduce.3.cloned.1.call-start = ((), (), s32[]{:S(2)}) async-start(), calls=%async_computation.7 | async-start | bytes 933888 | tf_op jit(solution)/shard_map/psum | solution.py:141
  212.0 278.1 %all-reduce.5.cloned.1.call-start = ((), (), s32[]{:S(2)}) async-start(), calls=%async_computation.8 | async-start | bytes 933888 | tf_op jit(solution)/shard_map/psum | solution.py:141
  332.2 192.7 %all-to-all-start.6 = ((f32[16,128,300]{1,2,0:T(8,128)}), f32[16,128,300]{1,2,0:T(8,128)S(1)}, u32[]{:S(2)}, u32[]{:S(2)}) async-start(f32[16,128,300]{1,2,0:T(8,128)} %copy.60), calls=%async_computation.6 | async-start | bytes 4980736 | tf_op jit(solution)/shard_map/all_to_all | solution.py:85
  497.1 26.8 %copy-start = (bf16[128,300]{0,1:T(8,128)(2,1)S(1)}, bf16[128,300]{0,1:T(8,128)(2,1)}, u32[]{:S(2)}) copy-start(bf16[128,300]{0,1:T(8,128)(2,1)} %param.2) | copy-start | bytes 230404
Sparse Core Ops, SparseCore 0:
  212.1 117.6 all-reduce.2
  332.4 157.5 all-reduce.4
